TPU v7x, 32 devices: a whole 2x2x4 slice. The times are simulated.
32 devices in a mesh: gx: 8 (over y, x, core), gy: 4 (over z).
Axes of the slice: x: 2, y: 2, z: 4, core: 2. Of those that a mesh axis runs over, the one named last changes fastest.
Arguments:
- layer_early: bfloat16 [1024, 8192], P(None, ('gx', 'gy')), may hold values from -48 to 48
- layer_late: bfloat16 [1024, 8192], P(('gx', 'gy')), may hold values from -48 to 48
Outputs:
- similarity: float32 [], replicated
- token_share: float32 [1024], P(('gx', 'gy'))
- early_rows: bfloat16 [1024, 8192], P(('gx', 'gy'))
- late_rows: bfloat16 [1024, 8192], P(('gx', 'gy'))
All inputs are finite; a program needn't handle non-finite values.
Results may differ from a plain program's by a relative error of at most 0.0015.
Values may be sent and summed in bfloat16 or wider, within the bound.
A program may use at most 128 MiB of HBM per device.

v0:
```python
import jax
import jax.numpy as jnp
from jax import lax
from jax.sharding import PartitionSpec as P


def pair_terms(left_early, left_late, right_early, right_late):
    dims = (((1,), (1,)), ((), ()))
    block_early = lax.dot_general(left_early, right_early, dims, preferred_element_type=jnp.float32)
    block_late = lax.dot_general(left_late, right_late, dims, preferred_element_type=jnp.float32)
    return (
        jnp.sum(block_early * block_late, axis=1),
        jnp.sum(block_early * block_early),
        jnp.sum(block_late * block_late),
    )


def body(layer_early, layer_late):
    total_rows = layer_early.shape[0]
    early_values = layer_early.astype(jnp.float32)
    early_cols = (early_values - jnp.mean(early_values, axis=0)).astype(jnp.bfloat16)
    late_values = layer_late.astype(jnp.float32)
    column_sums = lax.psum(jnp.sum(late_values, axis=0), ("gx", "gy"))
    late_rows = (late_values - column_sums / total_rows).astype(jnp.bfloat16)
    early_rows = lax.all_to_all(early_cols, ("gx", "gy"), split_axis=0, concat_axis=1, tiled=True)
    block_early, block_late = (
        lax.all_gather(early_rows, "gy", axis=0, tiled=True),
        lax.all_gather(late_rows, "gy", axis=0, tiled=True),
    )
    row_part, early_part, late_part = pair_terms(
        block_early,
        block_late,
        lax.all_gather(early_rows, "gx", axis=0, tiled=True),
        lax.all_gather(late_rows, "gx", axis=0, tiled=True),
    )
    own_align = lax.psum_scatter(row_part, "gy", scatter_dimension=0, tiled=True)
    total_kl, total_kk, total_ll = lax.psum(
        (jnp.sum(row_part), early_part, late_part), ("gx", "gy")
    )
    scale_norm = jnp.sqrt(total_kk * total_ll)
    similarity = total_kl / scale_norm
    token_share = total_rows * own_align / scale_norm
    return (similarity, token_share, early_rows, late_rows)


def solution(mesh):
    in_specs = (P(None, ("gx", "gy")), P(("gx", "gy"), None))
    out_specs = (P(), P(("gx", "gy")), P(("gx", "gy"), None), P(("gx", "gy"), None))
    return jax.shard_map(body, mesh=mesh, in_specs=in_specs, out_specs=out_specs, check_vma=False)
```

profile of v0, /device:TPU:0, one launch (start us, length us, event | category | flops | bytes accessed | tf_op | source)
XLA Modules:
  0.0 298.2 jit_solution(8457581897998979989)
XLA Ops:
  7.2 0.0 all-gather.9.cloned.1.call-start
  7.2 1.2 convert_reduce_fusion
  8.4 42.1 %psum.28 = f32[8192]{0:T(1024)S(1)} all-reduce(f32[8192]{0:T(1024)S(1)} %convert_reduce_fusion), channel_id=1, replica_groups=mesh['gx'=8,'gy'=4] {'gx','gy'}, use_global_device_ids=true, to_apply=%region_2.0 | all-reduce | flops 8192 | bytes 65536 | tf_op jit(solution)/shard_map/psum | solution.py:23
  50.6 1.9 fusion.1
  52.5 0.0 all-gather.9.cloned.1.call-update
  52.5 0.0 all-gather.11.cloned.1.call-start
  52.5 0.7 all-gather.11.cloned.1.call-update
  53.3 0.0 all-gather.5.cloned.1.call-start
  53.3 1.2 convert_reduce_fusion.1
  54.5 1.1 fusion
  55.6 28.2 %all_to_all.19 = bf16[32,32,256]{2,1,0:T(8,128)(2,1)S(1)} all-to-all(bf16[32,32,256]{2,1,0:T(8,128)(2,1)S(1)} %bitcast.12), channel_id=1, replica_groups=mesh['gx'=8,'gy'=4] {'gx','gy'}, dimensions={0} | all-to-all | bytes 1048576 | tf_op jit(solution)/shard_map/all_to_all | solution.py:25
  83.9 0.8 copy.8
  84.7 0.0 all-gather.7.cloned.1.call-start
  84.8 0.5 all-gather.7.cloned.1.call-update
  85.3 0.6 dynamic-slice
  86.6 22.4 %all-gather.9.cloned.1.call-done = bf16[128,8192]{1,0:T(8,128)(2,1)} async-done(((bf16[32,8192]{1,0:T(8,128)(2,1)}), bf16[128,8192]{1,0:T(8,128)(2,1)}) %all-gather.9.cloned.1.call-update) | async-done | bytes 2097168 | tf_op jit(solution)/shard_map/all_gather | solution.py:28
  109.0 38.1 %all-gather.11.cloned.1.call-done = bf16[256,8192]{1,0:T(8,128)(2,1)} async-done(((bf16[32,8192]{1,0:T(8,128)(2,1)}), bf16[256,8192]{1,0:T(8,128)(2,1)}) %all-gather.11.cloned.1.call-update) | async-done | bytes 4194320 | tf_op jit(solution)/shard_map/all_gather | solution.py:34
  147.1 4.4 %fusion.3 = f32[128,256]{1,0:T(8,128)S(1)} fusion(bf16[128,8192]{1,0:T(8,128)(2,1)} %all-gather.9.cloned.1.call-done, bf16[256,8192]{1,0:T(8,128)(2,1)} %all-gather.11.cloned.1.call-done), kind=kOutput, calls=%fused_computation.14 | convolution fusion | flops 536870912 | bytes 6422528 | tf_op jit(solution)/shard_map/dot_general | solution.py:10
  151.5 43.5 %all-gather.5.cloned.1.call-done = bf16[128,8192]{1,0:T(8,128)(2,1)} async-done(((bf16[32,8192]{1,0:T(8,128)(2,1)}), bf16[128,8192]{1,0:T(8,128)(2,1)}) %all-gather.5.cloned.1.call-update) | async-done | bytes 2097168 | tf_op jit(solution)/shard_map/all_gather | solution.py:27
  195.0 37.7 %all-gather.7.cloned.1.call-done = bf16[256,8192]{1,0:T(8,128)(2,1)} async-done(((bf16[32,8192]{1,0:T(8,128)(2,1)}), bf16[256,8192]{1,0:T(8,128)(2,1)}) %all-gather.7.cloned.1.call-update) | async-done | bytes 4194320 | tf_op jit(solution)/shard_map/all_gather | solution.py:33
  232.7 5.0 %multiply_reduce_fusion.2 = (f32[128]{0:T(128)S(1)}, f32[]{:T(128)}, f32[]{:T(128)}, f32[]{:T(128)}) fusion(f32[128,256]{1,0:T(8,128)S(1)} %fusion.3, bf16[128,8192]{1,0:T(8,128)(2,1)} %all-gather.5.cloned.1.call-done, bf16[256,8192]{1,0:T(8,128)(2,1)} %all-gather.7.cloned.1.call-done), kind=kOutput, calls=%fused_computation.8 | convolution fusion | flops 537100160 | bytes 6423052 | tf_op jit(solution)/shard_map/dot_general | solution.py:9
  237.7 39.6 %all-reduce.1 = (f32[]{:T(128)}, f32[]{:T(128)}, f32[]{:T(128)}) all-reduce(f32[]{:T(128)} %get-tuple-element.5, f32[]{:T(128)} %get-tuple-element.7, f32[]{:T(128)} %get-tuple-element.6), channel_id=1, replica_groups=mesh['gx'=8,'gy'=4] {'gx','gy'}, use_global_device_ids=true, to_apply=%region_4.0 | all-reduce | flops 3 | bytes 24 | tf_op jit(solution)/shard_map/psum | solution.py:37
  278.7 10.6 %all-reduce = f32[128]{0:T(128)S(1)} all-reduce(f32[128]{0:T(128)S(1)} %get-tuple-element.4), channel_id=2, replica_groups=mesh['gx'=8,'gy'=4] {'gy'}, use_global_device_ids=true, to_apply=%region_10.0.clone | all-reduce | flops 128 | bytes 1024
  290.0 0.6 fusion.2
  (5 shorter events, 0.0 us)
Async XLA Ops:
  7.2 78.2 %copy-start = (u32[32]{0:T(128)S(1)}, u32[32]{0:T(128)}, u32[]{:S(2)}) copy-start(u32[32]{0:T(128)} %constant.11) | copy-start | bytes 388
  7.2 101.8 %all-gather.9.cloned.1.call-start = ((), (), s32[]{:S(2)}) async-start(), calls=%async_computation.3 | async-start | bytes 2621440 | tf_op jit(solution)/shard_map/all_gather | solution.py:28
  52.5 94.6 %all-gather.11.cloned.1.call-start = ((), (), s32[]{:S(2)}) async-start(), calls=%async_computation.4 | async-start | bytes 4718592 | tf_op jit(solution)/shard_map/all_gather | solution.py:34
  53.3 141.7 %all-gather.5.cloned.1.call-start = ((), (), s32[]{:S(2)}) async-start(), calls=%async_computation.1 | async-start | bytes 2621440 | tf_op jit(solution)/shard_map/all_gather | solution.py:27
  84.7 147.9 %all-gather.7.cloned.1.call-start = ((), (), s32[]{:S(2)}) async-start(), calls=%async_computation.2 | async-start | bytes 4718592 | tf_op jit(solution)/shard_map/all_gather | solution.py:33
Sparse Core Ops, SparseCore 0:
  52.6 56.3 all-gather.8
  111.5 35.5 all-gather.10
  149.3 45.6 all-gather.4
  197.3 35.3 all-gather.6
where the time goes:
time: 299 us; the launch traced here: 298 us
  waiting for transfers between devices  143 us (48%)
  blocking collectives  121 us (40%)
  between operations  17.6 us (6%)
  matrix products  9.4 us (3%)
  other arithmetic  6.03 us (2%)
    all_gather x1, waiting for transfers between devices, body(): lax.all_gather(early_rows, 'gy', axis=0, tiled=True)  43.5 us
    psum x1, blocking collectives, body(): column_sums = lax.psum(jnp.sum(late_values, axis=0), ('gx', 'gy'))  42.1 us
    psum x1, blocking collectives, body(): lax.psum((jnp.sum(row_part), early_part, late_part), ('gx', 'gy'))  39.6 us
    all_gather x1, waiting for transfers between devices, body(): lax.all_gather(late_rows, 'gx', axis=0, tiled=True)  38.1 us
    all_gather x1, waiting for transfers between devices, body(): lax.all_gather(early_rows, 'gx', axis=0, tiled=True)  37.7 us
    all_to_all x1, blocking collectives, body(): lax.all_to_all(early_cols, ('gx', 'gy'), split_axis=0, concat_axis=1, til...  28.2 us
    all_gather x1, waiting for transfers between devices, body(): lax.all_gather(late_rows, 'gy', axis=0, tiled=True)  22.4 us
    unnamed x1, blocking collectives  10.6 us
  transfers between devices with their start and end apart: 4, of which 4 were waited for; matrix products, arithmetic and copies ran while one was open for 3% of the time, Pallas kernels for 0%

commit v1 on v0

--- a/solution.py
+++ b/solution.py
@@ -1,13 +1,20 @@
+import functools
+
 import jax
 import jax.numpy as jnp
 from jax import lax
+from jax.experimental import pallas as pl
+from jax.experimental.pallas import tpu as pltpu
 from jax.sharding import PartitionSpec as P
 
+MESH = pl.DeviceIdType.MESH
+NT = (((1,), (1,)), ((), ()))
+VMEM_BUDGET = 48 * 2**20
+
 
 def pair_terms(left_early, left_late, right_early, right_late):
-    dims = (((1,), (1,)), ((), ()))
-    block_early = lax.dot_general(left_early, right_early, dims, preferred_element_type=jnp.float32)
-    block_late = lax.dot_general(left_late, right_late, dims, preferred_element_type=jnp.float32)
+    block_early = lax.dot_general(left_early, right_early, NT, preferred_element_type=jnp.float32)
+    block_late = lax.dot_general(left_late, right_late, NT, preferred_element_type=jnp.float32)
     return (
         jnp.sum(block_early * block_late, axis=1),
         jnp.sum(block_early * block_early),
@@ -15,7 +22,7 @@
     )
 
 
-def body(layer_early, layer_late):
+def gather_body(layer_early, layer_late):
     total_rows = layer_early.shape[0]
     early_values = layer_early.astype(jnp.float32)
     early_cols = (early_values - jnp.mean(early_values, axis=0)).astype(jnp.bfloat16)
@@ -43,7 +50,249 @@
     return (similarity, token_share, early_rows, late_rows)
 
 
+def kernel(gx, gy, early_ref, late_ref, early_out, late_out, small_out,
+           early_pair, late_pair, means,
+           early_send, early_recv, early_own, late_send, late_recv, late_own,
+           early_zsend, early_zrecv, late_zsend, late_zrecv,
+           msg, msg_recv,
+           a2a_send, a2a_recv, own_sem, pair_send, pair_recv, mean_send, mean_recv,
+           plane_send, plane_recv, z_send, z_recv, msg_send, msg_recv_sem):
+    n = gx * gy
+    tokens, cols = early_ref.shape
+    rows = late_ref.shape[0]
+    block = tokens // gx
+    half = gx // 2
+    x, y = lax.axis_index("gx"), lax.axis_index("gy")
+    me = x * gy + y
+    core = lax.rem(x, 2)
+    chip = x // 2
+    partner = x + 1 - 2 * core
+
+    def device(t):
+        return (t // gy, lax.rem(t, gy))
+
+    def lanes(i):
+        return pl.ds(pl.multiple_of(i * cols, cols), cols)
+
+    def tile_rows(i, size):
+        return pl.ds(pl.multiple_of(i * size, size), size)
+
+    def others(f):
+        def step(o, carry):
+            f(lax.rem(me + o, n))
+            return carry
+        lax.fori_loop(1, n, step, 0)
+
+    def wait_bytes(ref, sem):
+        pltpu.make_async_copy(ref, ref, sem).wait()
+
+    barrier = pltpu.get_barrier_semaphore()
+    others(lambda t: pl.semaphore_signal(barrier, inc=1, device_id=device(t), device_id_type=MESH))
+    pl.semaphore_wait(barrier, n - 1)
+
+    own_rows = tile_rows(me, rows)
+
+    others(lambda t: pltpu.make_async_remote_copy(
+        src_ref=late_ref.at[:, lanes(t)], dst_ref=late_pair.at[own_rows, pl.ds(0, cols)],
+        send_sem=a2a_send.at[0], recv_sem=a2a_recv.at[0],
+        device_id=device(t), device_id_type=MESH).start())
+    late_pair[own_rows, pl.ds(0, cols)] = late_ref[:, lanes(me)]
+
+    values = early_ref[...].astype(jnp.float32)
+    mean = jnp.sum(values, axis=0, keepdims=True) / tokens
+    early_pair[:, pl.ds(0, cols)] = (values - mean).astype(jnp.bfloat16)
+
+    def swap(pair, i):
+        return pltpu.make_async_remote_copy(
+            src_ref=pair.at[:, pl.ds(0, cols)], dst_ref=pair.at[:, pl.ds(cols, cols)],
+            send_sem=pair_send.at[i], recv_sem=pair_recv.at[i],
+            device_id=(partner, y), device_id_type=MESH)
+
+    early_swap = swap(early_pair, 0)
+    early_swap.start()
+
+    def gram_pieces(pair, own, send, recv, i):
+        copies = []
+        for o in list(range(1, half)) + [0]:
+            q = 2 * lax.rem(chip + o, half) + core
+            left = pair[tile_rows(q, block), :]
+            right = jnp.concatenate(
+                [pair[tile_rows(lax.rem(q + d, gx), block), :] for d in range(half + 1)], axis=0)
+            piece = lax.dot_general(left, right, NT, preferred_element_type=jnp.float32)
+            if o == 0:
+                own[...] = piece
+            else:
+                send[o - 1] = piece.astype(jnp.bfloat16)
+                copy = pltpu.make_async_remote_copy(
+                    src_ref=send.at[o - 1], dst_ref=recv.at[o - 1],
+                    send_sem=plane_send.at[i, o - 1], recv_sem=plane_recv.at[i, o - 1],
+                    device_id=(q, y), device_id_type=MESH)
+                copy.start()
+                copies.append(copy)
+        return copies
+
+    def along_z(copies, own, recv, zsend, zrecv, i):
+        total = own[...]
+        for o, copy in enumerate(copies):
+            copy.wait_recv()
+            total = total + recv[o].astype(jnp.float32)
+        own[...] = total
+        zsend[...] = total.astype(jnp.bfloat16)
+        out = []
+        for o in range(1, gy):
+            z = lax.rem(y + o, gy)
+            copy = pltpu.make_async_remote_copy(
+                src_ref=zsend.at[tile_rows(z, rows), :], dst_ref=zrecv.at[o - 1],
+                send_sem=z_send.at[i, o - 1], recv_sem=z_recv.at[i, o - 1],
+                device_id=(x, z), device_id_type=MESH)
+            copy.start()
+            out.append(copy)
+        return out
+
+    early_swap.wait_recv()
+    early_copies = gram_pieces(early_pair, early_own, early_send, early_recv, 0)
+
+    others(lambda t: pltpu.make_async_remote_copy(
+        src_ref=early_pair.at[tile_rows(t, rows), pl.ds(0, cols)], dst_ref=early_out.at[:, lanes(me)],
+        send_sem=a2a_send.at[1], recv_sem=a2a_recv.at[1],
+        device_id=device(t), device_id_type=MESH).start())
+    own_copy = pltpu.make_async_copy(
+        early_pair.at[own_rows, pl.ds(0, cols)], early_out.at[:, lanes(me)], own_sem)
+    own_copy.start()
+
+    wait_bytes(late_pair.at[pl.ds(0, tokens - rows), pl.ds(0, cols)], a2a_recv.at[0])
+    values = late_pair[:, pl.ds(0, cols)].astype(jnp.float32)
+    mean = jnp.sum(values, axis=0, keepdims=True) / tokens
+    late_pair[:, pl.ds(0, cols)] = (values - mean).astype(jnp.bfloat16)
+    late_swap = swap(late_pair, 1)
+    late_swap.start()
+    means[:, lanes(me)] = mean
+    others(lambda t: pltpu.make_async_remote_copy(
+        src_ref=means.at[:, lanes(me)], dst_ref=means.at[:, lanes(me)],
+        send_sem=mean_send, recv_sem=mean_recv,
+        device_id=device(t), device_id_type=MESH).start())
+
+    late_swap.wait_recv()
+    late_copies = gram_pieces(late_pair, late_own, late_send, late_recv, 1)
+    early_z = along_z(early_copies, early_own, early_recv, early_zsend, early_zrecv, 0)
+    wait_bytes(means.at[:, pl.ds(0, (n - 1) * cols)], mean_recv)
+    late_out[...] = (late_ref[...].astype(jnp.float32) - means[...]).astype(jnp.bfloat16)
+    late_z = along_z(late_copies, late_own, late_recv, late_zsend, late_zrecv, 1)
+
+    def final(copies, own, zrecv):
+        total = own[tile_rows(y, rows), :]
+        for o, copy in enumerate(copies):
+            copy.wait_recv()
+            total = total + zrecv[o].astype(jnp.float32)
+        return total
+
+    k = final(early_z, early_own, early_zrecv)
+    l = final(late_z, late_own, late_zrecv)
+    kl = k * l
+    sub = lax.broadcasted_iota(jnp.int32, (rows, block), 0)
+    lane = lax.broadcasted_iota(jnp.int32, (rows, block), 1)
+
+    def weighted(v):
+        doubled = jnp.sum(v[:, block:half * block])
+        return jnp.sum(v[:, :block]) + jnp.sum(v[:, half * block:]) + 2.0 * doubled
+
+    head = lax.broadcasted_iota(jnp.int32, (1, block), 1)
+    scalars = jnp.where(head == 0, weighted(kl), jnp.where(
+        head == 1, weighted(k * k), jnp.where(head == 2, weighted(l * l), 0.0)))
+    for d in range(gx):
+        if 0 < d < half:
+            top = jnp.sum(kl[:, d * block:(d + 1) * block], axis=0, keepdims=True)
+        else:
+            top = jnp.zeros((1, block), jnp.float32)
+        msg[d] = jnp.concatenate([top, scalars], axis=0)
+    msg_recv[me] = msg[0]
+    others(lambda t: pltpu.make_async_remote_copy(
+        src_ref=msg.at[lax.rem(t // gy - x + gx, gx)], dst_ref=msg_recv.at[me],
+        send_sem=msg_send, recv_sem=msg_recv_sem,
+        device_id=device(t), device_id_type=MESH).start())
+    own_align = jnp.sum(kl, axis=1, keepdims=True)
+    wait_bytes(msg_recv.at[pl.ds(0, n - 1)], msg_recv_sem)
+    got = jnp.sum(msg_recv[...], axis=0)
+    below = jnp.sum(jnp.where(lane == y * rows + sub, got[0:1, :], 0.0), axis=1, keepdims=True)
+    align = jnp.sum(jnp.where(lane == sub, own_align + below, 0.0), axis=0, keepdims=True)
+    sums = got[1:2, :]
+    total_kl = jnp.sum(jnp.where(head == 0, sums, 0.0), axis=1, keepdims=True)
+    total_kk = jnp.sum(jnp.where(head == 1, sums, 0.0), axis=1, keepdims=True)
+    total_ll = jnp.sum(jnp.where(head == 2, sums, 0.0), axis=1, keepdims=True)
+    scale_norm = jnp.sqrt(total_kk * total_ll)
+    small_out[0:1, :] = tokens * align / scale_norm
+    small_out[1:2, :] = jnp.broadcast_to(total_kl / scale_norm, (1, block))
+
+    part = late_pair.at[pl.ds(0, tokens - rows), pl.ds(0, cols)]
+    wait_bytes(part, a2a_send.at[0])
+    wait_bytes(part, a2a_send.at[1])
+    wait_bytes(early_out.at[:, pl.ds(0, (n - 1) * cols)], a2a_recv.at[1])
+    own_copy.wait()
+    early_swap.wait_send()
+    late_swap.wait_send()
+    wait_bytes(means.at[:, pl.ds(0, (n - 1) * cols)], mean_send)
+    wait_bytes(msg_recv.at[pl.ds(0, n - 1)], msg_send)
+    for copy in early_copies + late_copies + early_z + late_z:
+        copy.wait_send()
+
+
+def exchange_body(gx, gy, layer_early, layer_late):
+    tokens, cols = layer_early.shape
+    rows, width = layer_late.shape
+    n = gx * gy
+    block = tokens // gx
+    half = gx // 2
+    span = (half + 1) * block
+    bf16, f32 = jnp.bfloat16, jnp.float32
+    dma = pltpu.SemaphoreType.DMA
+    gram = [
+        pltpu.VMEM((half - 1, block, span), bf16),
+        pltpu.VMEM((half - 1, block, span), bf16),
+        pltpu.VMEM((block, span), f32),
+    ]
+    z_part = [pltpu.VMEM((block, span), bf16), pltpu.VMEM((gy - 1, rows, span), bf16)]
+    vmem = pl.BlockSpec(memory_space=pltpu.VMEM)
+    early_rows, late_rows, small = pl.pallas_call(
+        functools.partial(kernel, gx, gy),
+        out_shape=(
+            jax.ShapeDtypeStruct((rows, width), bf16),
+            jax.ShapeDtypeStruct((rows, width), bf16),
+            jax.ShapeDtypeStruct((2, block), f32),
+        ),
+        in_specs=[vmem, vmem],
+        out_specs=(pl.BlockSpec(memory_space=pl.ANY), vmem, vmem),
+        scratch_shapes=[
+            pltpu.VMEM((tokens, 2 * cols), bf16),
+            pltpu.VMEM((tokens, 2 * cols), bf16),
+            pltpu.VMEM((1, width), f32),
+            *gram, *gram, *z_part, *z_part,
+            pltpu.VMEM((gx, 2, block), f32),
+            pltpu.VMEM((n, 2, block), f32),
+            dma((2,)), dma((2,)), dma, dma((2,)), dma((2,)), dma, dma,
+            dma((2, half - 1)), dma((2, half - 1)), dma((2, gy - 1)), dma((2, gy - 1)), dma, dma,
+        ],
+        compiler_params=pltpu.CompilerParams(collective_id=0, has_side_effects=True),
+    )(layer_early, layer_late)
+    return small[1, 0], small[0, :rows], early_rows, late_rows
+
+
+def fits(gx, gy, tokens, width):
+    n = gx * gy
+    cols, rows, block = width // n, tokens // n, tokens // gx
+    aligned = cols % 128 == 0 and rows % 16 == 0 and block % 128 == 0
+    span = (gx // 2 + 1) * block
+    held = 12 * tokens * cols + 4 * gx * block * span + 24 * block * span
+    return gx % 2 == 0 and gx >= 4 and gy >= 2 and aligned and rows <= block and held <= VMEM_BUDGET
+
+
 def solution(mesh):
+    gx, gy = mesh.shape["gx"], mesh.shape["gy"]
+
+    def body(layer_early, layer_late):
+        if fits(gx, gy, layer_early.shape[0], layer_late.shape[1]):
+            return exchange_body(gx, gy, layer_early, layer_late)
+        return gather_body(layer_early, layer_late)
+
     in_specs = (P(None, ("gx", "gy")), P(("gx", "gy"), None))
     out_specs = (P(), P(("gx", "gy")), P(("gx", "gy"), None), P(("gx", "gy"), None))
     return jax.shard_map(body, mesh=mesh, in_specs=in_specs, out_specs=out_specs, check_vma=False)

time: 299 us -> 55.5 us (0.19)
  waiting for transfers between devices: 143 us -> 0 us
  blocking collectives: 121 us -> 0 us
  Pallas kernels: 0 us -> 50.3 us
  between operations: 17.6 us -> 0.65 us
  matrix products: 9.4 us -> 0 us
  other arithmetic: 6.03 us -> 0 us
  local copies, waits for them, and re-layouts: 1.42 us -> 4.41 us
    all_gather x4 -> x0, waiting for transfers between devices: 142 us -> none  [the longest x1 43.5 us: body(): lax.all_gather(early_rows, 'gy', axis=0, tiled=True)]
    psum x2 -> x0, blocking collectives: 81.7 us -> none  [the longest x1 42.1 us: body(): column_sums = lax.psum(jnp.sum(late_values, axis=0), ('gx', 'gy'))]
    pallas_call x0 -> x1, Pallas kernels: none -> 50.3 us  [exchange_body(): pl.pallas_call(functools.partial(kernel, gx, gy), out_shape=(jax.ShapeDty...]
    all_to_all x1 -> x0, blocking collectives: 28.2 us -> none  [body(): lax.all_to_all(early_cols, ('gx', 'gy'), split_axis=0, concat_axis=1, til...]
    unnamed x1 -> x0, blocking collectives: 10.6 us -> none
    dot_general x2 -> x0, matrix products: 9.4 us -> none  [the longest x1 5.05 us: pair_terms(): lax.dot_general(left_early, right_early, dims, preferred_element_type=jnp...]
    convert_element_type x2 -> x0, other arithmetic: 3.07 us -> none  [the longest x1 1.92 us: body(): late_rows = (late_values - column_sums / total_rows).astype(jnp.bfloat16)]
  transfers between devices with their start and end apart: 4 -> 0, of which waited for: 4 -> 0; matrix products, arithmetic and copies ran while one was open for 3% -> 0% of each run, Pallas kernels for 0% -> 0%
where the time goes in v1:
time: 55.5 us; the launch traced here: 55.4 us
  Pallas kernels  50.3 us (91%)
  local copies, waits for them, and re-layouts  4.41 us (8%)
  between operations  0.65 us (1%)
    pallas_call x1, Pallas kernels, exchange_body(): pl.pallas_call(functools.partial(kernel, gx, gy), out_shape=(jax.ShapeDty...  50.3 us
    unnamed x6, local copies, waits for them, and re-layouts  3.38 us

profile of v1, /device:TPU:0, one launch (start us, length us, event | category | flops | bytes accessed | tf_op | source)
XLA Modules:
  0.0 55.4 jit_solution(13635730446133089081)
XLA Ops:
  0.6 50.3 %shard_map.57 = (bf16[32,8192]{1,0:T(8,128)(2,1)}, bf16[32,8192]{1,0:T(8,128)(2,1)}, f32[2,128]{1,0:T(2,128)}) custom-call(bf16[1024,256]{1,0:T(8,128)(2,1)} %early_ref.1, bf16[32,8192]{1,0:T(8,128)(2,1)} %late_ref.1), custom_call_target="tpu_custom_call" | custom-call | tf_op jit(solution)/shard_map/pallas_call | solution.py:255
  50.9 0.0 copy-start.1
  51.0 0.7 %copy-done.1 = f32[2,128]{1,0:T(2,128)S(1)} copy-done((f32[2,128]{1,0:T(2,128)S(1)}, f32[2,128]{1,0:T(2,128)}, u32[]{:S(2)}) %copy-start.1) | copy-done | bytes 1048
  51.6 0.5 slice.6
  52.1 0.5 slice_bitcast_fusion
  52.6 0.0 copy-start
  52.6 1.9 %copy.8 = bf16[32,8192]{1,0:T(8,128)(2,1)} copy(bf16[32,8192]{1,0:T(8,128)(2,1)} %get-tuple-element.16) | data formatting | bytes 1048576
  54.6 0.0 copy-done
  54.6 0.8 %copy.9 = bf16[32,8192]{1,0:T(8,128)(2,1)} copy(bf16[32,8192]{1,0:T(8,128)(2,1)S(1)} %copy-done) | data formatting | bytes 1048576
Async XLA Ops:
  50.9 0.7 %copy-start.1 = (f32[2,128]{1,0:T(2,128)S(1)}, f32[2,128]{1,0:T(2,128)}, u32[]{:S(2)}) copy-start(f32[2,128]{1,0:T(2,128)} %get-tuple-element.7) | copy-start | bytes 3076
  52.6 1.9 %copy-start = (bf16[32,8192]{1,0:T(8,128)(2,1)S(1)}, bf16[32,8192]{1,0:T(8,128)(2,1)}, u32[]{:S(2)}) copy-start(bf16[32,8192]{1,0:T(8,128)(2,1)} %get-tuple-element.17) | copy-start | bytes 1572868

commit v2 on v1

--- a/solution.py
+++ b/solution.py
@@ -50,13 +50,15 @@
     return (similarity, token_share, early_rows, late_rows)
 
 
-def kernel(gx, gy, early_ref, late_ref, early_out, late_out, small_out,
-           early_pair, late_pair, means,
+def kernel(gx, gy, early_hbm, late_hbm, early_out, early_mean_out, late_mean_out, share_out, similarity_out,
+           early_ref, late_ref, early_plane, early_pair, late_pair, means,
            early_send, early_recv, early_own, late_send, late_recv, late_own,
            early_zsend, early_zrecv, late_zsend, late_zrecv,
+           diag_send, diag_recv, diag_zsend, diag_zrecv,
            msg, msg_recv,
-           a2a_send, a2a_recv, own_sem, pair_send, pair_recv, mean_send, mean_recv,
-           plane_send, plane_recv, z_send, z_recv, msg_send, msg_recv_sem):
+           stage_sem, a2a_send, a2a_recv, own_sem, pair_send, pair_recv, mean_send, mean_recv,
+           plane_send, plane_recv, z_send, z_recv, msg_send, msg_recv_sem,
+           diag_plane_send, diag_plane_recv, diag_z_send, diag_z_recv, out_send, out_recv):
     n = gx * gy
     tokens, cols = early_ref.shape
     rows = late_ref.shape[0]
@@ -88,6 +90,11 @@
 
     barrier = pltpu.get_barrier_semaphore()
     others(lambda t: pl.semaphore_signal(barrier, inc=1, device_id=device(t), device_id_type=MESH))
+    stage_late = pltpu.make_async_copy(late_hbm, late_ref, stage_sem.at[0])
+    stage_late.start()
+    stage_early = pltpu.make_async_copy(early_hbm, early_ref, stage_sem.at[1])
+    stage_early.start()
+    stage_late.wait()
     pl.semaphore_wait(barrier, n - 1)
 
     own_rows = tile_rows(me, rows)
@@ -98,9 +105,21 @@
         device_id=device(t), device_id_type=MESH).start())
     late_pair[own_rows, pl.ds(0, cols)] = late_ref[:, lanes(me)]
 
+    stage_early.wait()
+    plane_copies = []
+    for o in range(1, gx):
+        p = lax.rem(x + o, gx)
+        copy = pltpu.make_async_remote_copy(
+            src_ref=early_ref.at[tile_rows(p, block), :], dst_ref=early_plane.at[:, lanes(x)],
+            send_sem=out_send.at[o - 1], recv_sem=out_recv.at[o - 1],
+            device_id=(p, y), device_id_type=MESH)
+        copy.start()
+        plane_copies.append(copy)
+    early_plane[:, lanes(x)] = early_ref[tile_rows(x, block), :]
+
     values = early_ref[...].astype(jnp.float32)
-    mean = jnp.sum(values, axis=0, keepdims=True) / tokens
-    early_pair[:, pl.ds(0, cols)] = (values - mean).astype(jnp.bfloat16)
+    early_mean = jnp.sum(values, axis=0, keepdims=True) / tokens
+    early_pair[:, pl.ds(0, cols)] = (values - early_mean).astype(jnp.bfloat16)
 
     def swap(pair, i):
         return pltpu.make_async_remote_copy(
@@ -111,8 +130,13 @@
     early_swap = swap(early_pair, 0)
     early_swap.start()
 
+    def diagonal(v):
+        on = (lax.broadcasted_iota(jnp.int32, (block, block), 0)
+              == lax.broadcasted_iota(jnp.int32, (block, block), 1))
+        return jnp.sum(jnp.where(on, v[:, :block], 0.0), axis=0, keepdims=True)
+
     def gram_pieces(pair, own, send, recv, i):
-        copies = []
+        copies, diag_copies = [], []
         for o in list(range(1, half)) + [0]:
             q = 2 * lax.rem(chip + o, half) + core
             left = pair[tile_rows(q, block), :]
@@ -122,6 +146,13 @@
             if o == 0:
                 own[...] = piece
             else:
+                diag_send[i, o - 1] = diagonal(piece)
+                copy = pltpu.make_async_remote_copy(
+                    src_ref=diag_send.at[i, o - 1], dst_ref=diag_recv.at[i, o - 1],
+                    send_sem=diag_plane_send.at[i, o - 1], recv_sem=diag_plane_recv.at[i, o - 1],
+                    device_id=(q, y), device_id_type=MESH)
+                copy.start()
+                diag_copies.append(copy)
                 send[o - 1] = piece.astype(jnp.bfloat16)
                 copy = pltpu.make_async_remote_copy(
                     src_ref=send.at[o - 1], dst_ref=recv.at[o - 1],
@@ -129,36 +160,39 @@
                     device_id=(q, y), device_id_type=MESH)
                 copy.start()
                 copies.append(copy)
-        return copies
+        return copies, diag_copies
 
     def along_z(copies, own, recv, zsend, zrecv, i):
+        copies, diag_copies = copies
         total = own[...]
-        for o, copy in enumerate(copies):
-            copy.wait_recv()
+        diag = diagonal(total)
+        for o in range(half - 1):
+            diag_copies[o].wait_recv()
+            diag = diag + diag_recv[i, o]
+            copies[o].wait_recv()
             total = total + recv[o].astype(jnp.float32)
         own[...] = total
         zsend[...] = total.astype(jnp.bfloat16)
-        out = []
+        diag_zsend[i] = diag
+        out, diag_out = [], []
         for o in range(1, gy):
             z = lax.rem(y + o, gy)
+            copy = pltpu.make_async_remote_copy(
+                src_ref=diag_zsend.at[i], dst_ref=diag_zrecv.at[i, o - 1],
+                send_sem=diag_z_send.at[i, o - 1], recv_sem=diag_z_recv.at[i, o - 1],
+                device_id=(x, z), device_id_type=MESH)
+            copy.start()
+            diag_out.append(copy)
             copy = pltpu.make_async_remote_copy(
                 src_ref=zsend.at[tile_rows(z, rows), :], dst_ref=zrecv.at[o - 1],
                 send_sem=z_send.at[i, o - 1], recv_sem=z_recv.at[i, o - 1],
                 device_id=(x, z), device_id_type=MESH)
             copy.start()
             out.append(copy)
-        return out
+        return out, diag_out
 
     early_swap.wait_recv()
     early_copies = gram_pieces(early_pair, early_own, early_send, early_recv, 0)
-
-    others(lambda t: pltpu.make_async_remote_copy(
-        src_ref=early_pair.at[tile_rows(t, rows), pl.ds(0, cols)], dst_ref=early_out.at[:, lanes(me)],
-        send_sem=a2a_send.at[1], recv_sem=a2a_recv.at[1],
-        device_id=device(t), device_id_type=MESH).start())
-    own_copy = pltpu.make_async_copy(
-        early_pair.at[own_rows, pl.ds(0, cols)], early_out.at[:, lanes(me)], own_sem)
-    own_copy.start()
 
     wait_bytes(late_pair.at[pl.ds(0, tokens - rows), pl.ds(0, cols)], a2a_recv.at[0])
     values = late_pair[:, pl.ds(0, cols)].astype(jnp.float32)
@@ -166,31 +200,50 @@
     late_pair[:, pl.ds(0, cols)] = (values - mean).astype(jnp.bfloat16)
     late_swap = swap(late_pair, 1)
     late_swap.start()
-    means[:, lanes(me)] = mean
+    means[:, lanes(me)] = jnp.concatenate([early_mean, mean], axis=0)
     others(lambda t: pltpu.make_async_remote_copy(
         src_ref=means.at[:, lanes(me)], dst_ref=means.at[:, lanes(me)],
         send_sem=mean_send, recv_sem=mean_recv,
         device_id=device(t), device_id_type=MESH).start())
 
+    for copy in plane_copies:
+        copy.wait_recv()
+    for o in range(1, gy):
+        z = lax.rem(y + o, gy)
+        for p in range(gx):
+            pltpu.make_async_remote_copy(
+                src_ref=early_plane.at[tile_rows(z, rows), pl.ds(p * cols, cols)],
+                dst_ref=early_out.at[:, lanes(p * gy + y)],
+                send_sem=a2a_send.at[1], recv_sem=a2a_recv.at[1],
+                device_id=(x, z), device_id_type=MESH).start()
+    for p in range(gx):
+        pltpu.make_async_copy(
+            early_plane.at[tile_rows(y, rows), pl.ds(p * cols, cols)],
+            early_out.at[:, lanes(p * gy + y)], own_sem).start()
+
     late_swap.wait_recv()
     late_copies = gram_pieces(late_pair, late_own, late_send, late_recv, 1)
+
     early_z = along_z(early_copies, early_own, early_recv, early_zsend, early_zrecv, 0)
-    wait_bytes(means.at[:, pl.ds(0, (n - 1) * cols)], mean_recv)
-    late_out[...] = (late_ref[...].astype(jnp.float32) - means[...]).astype(jnp.bfloat16)
     late_z = along_z(late_copies, late_own, late_recv, late_zsend, late_zrecv, 1)
 
-    def final(copies, own, zrecv):
+    def final(copies, own, zrecv, i):
+        copies, diag_copies = copies
         total = own[tile_rows(y, rows), :]
-        for o, copy in enumerate(copies):
-            copy.wait_recv()
+        diag = diag_zsend[i]
+        for o in range(gy - 1):
+            diag_copies[o].wait_recv()
+            diag = diag + diag_zrecv[i, o]
+            copies[o].wait_recv()
             total = total + zrecv[o].astype(jnp.float32)
-        return total
-
-    k = final(early_z, early_own, early_zrecv)
-    l = final(late_z, late_own, late_zrecv)
-    kl = k * l
+        first = jnp.where(lane == y * rows + sub, diag, total[:, :block])
+        return jnp.concatenate([first, total[:, block:]], axis=1)
+
     sub = lax.broadcasted_iota(jnp.int32, (rows, block), 0)
     lane = lax.broadcasted_iota(jnp.int32, (rows, block), 1)
+    k = final(early_z, early_own, early_zrecv, 0)
+    l = final(late_z, late_own, late_zrecv, 1)
+    kl = k * l
 
     def weighted(v):
         doubled = jnp.sum(v[:, block:half * block])
@@ -210,6 +263,9 @@
         src_ref=msg.at[lax.rem(t // gy - x + gx, gx)], dst_ref=msg_recv.at[me],
         send_sem=msg_send, recv_sem=msg_recv_sem,
         device_id=device(t), device_id_type=MESH).start())
+    wait_bytes(means.at[:, pl.ds(0, (n - 1) * cols)], mean_recv)
+    early_mean_out[...] = means[0:1, :]
+    late_mean_out[...] = means[1:2, :]
     own_align = jnp.sum(kl, axis=1, keepdims=True)
     wait_bytes(msg_recv.at[pl.ds(0, n - 1)], msg_recv_sem)
     got = jnp.sum(msg_recv[...], axis=0)
@@ -220,20 +276,23 @@
     total_kk = jnp.sum(jnp.where(head == 1, sums, 0.0), axis=1, keepdims=True)
     total_ll = jnp.sum(jnp.where(head == 2, sums, 0.0), axis=1, keepdims=True)
     scale_norm = jnp.sqrt(total_kk * total_ll)
-    small_out[0:1, :] = tokens * align / scale_norm
-    small_out[1:2, :] = jnp.broadcast_to(total_kl / scale_norm, (1, block))
+    share_out[...] = (tokens * align / scale_norm)[:, :rows]
+    similarity_out[...] = total_kl / scale_norm
 
     part = late_pair.at[pl.ds(0, tokens - rows), pl.ds(0, cols)]
     wait_bytes(part, a2a_send.at[0])
-    wait_bytes(part, a2a_send.at[1])
-    wait_bytes(early_out.at[:, pl.ds(0, (n - 1) * cols)], a2a_recv.at[1])
-    own_copy.wait()
+    for copy in plane_copies:
+        copy.wait_send()
+    wait_bytes(early_out.at[:, pl.ds(0, (gy - 1) * gx * cols)], a2a_send.at[1])
+    wait_bytes(early_out.at[:, pl.ds(0, (gy - 1) * gx * cols)], a2a_recv.at[1])
+    wait_bytes(early_out.at[:, pl.ds(0, gx * cols)], own_sem)
     early_swap.wait_send()
     late_swap.wait_send()
     wait_bytes(means.at[:, pl.ds(0, (n - 1) * cols)], mean_send)
     wait_bytes(msg_recv.at[pl.ds(0, n - 1)], msg_send)
-    for copy in early_copies + late_copies + early_z + late_z:
-        copy.wait_send()
+    for copies in (early_copies, late_copies, early_z, late_z):
+        for copy in copies[0] + copies[1]:
+            copy.wait_send()
 
 
 def exchange_body(gx, gy, layer_early, layer_late):
@@ -252,28 +311,42 @@
     ]
     z_part = [pltpu.VMEM((block, span), bf16), pltpu.VMEM((gy - 1, rows, span), bf16)]
     vmem = pl.BlockSpec(memory_space=pltpu.VMEM)
-    early_rows, late_rows, small = pl.pallas_call(
+    anywhere = pl.BlockSpec(memory_space=pl.ANY)
+    early_raw, early_mean, late_mean, share, similarity = pl.pallas_call(
         functools.partial(kernel, gx, gy),
         out_shape=(
             jax.ShapeDtypeStruct((rows, width), bf16),
-            jax.ShapeDtypeStruct((rows, width), bf16),
-            jax.ShapeDtypeStruct((2, block), f32),
+            jax.ShapeDtypeStruct((1, width), f32),
+            jax.ShapeDtypeStruct((1, width), f32),
+            jax.ShapeDtypeStruct((1, rows), f32),
+            jax.ShapeDtypeStruct((1, 1), f32),
         ),
-        in_specs=[vmem, vmem],
-        out_specs=(pl.BlockSpec(memory_space=pl.ANY), vmem, vmem),
+        in_specs=[anywhere, anywhere],
+        out_specs=(anywhere, vmem, vmem, vmem, vmem),
         scratch_shapes=[
+            pltpu.VMEM((tokens, cols), bf16),
+            pltpu.VMEM((rows, width), bf16),
+            pltpu.VMEM((block, gx * cols), bf16),
             pltpu.VMEM((tokens, 2 * cols), bf16),
             pltpu.VMEM((tokens, 2 * cols), bf16),
-            pltpu.VMEM((1, width), f32),
+            pltpu.VMEM((2, width), f32),
             *gram, *gram, *z_part, *z_part,
+            pltpu.VMEM((2, half - 1, 1, block), f32),
+            pltpu.VMEM((2, half - 1, 1, block), f32),
+            pltpu.VMEM((2, 1, block), f32),
+            pltpu.VMEM((2, gy - 1, 1, block), f32),
             pltpu.VMEM((gx, 2, block), f32),
             pltpu.VMEM((n, 2, block), f32),
-            dma((2,)), dma((2,)), dma, dma((2,)), dma((2,)), dma, dma,
+            dma((2,)), dma((2,)), dma((2,)), dma, dma((2,)), dma((2,)), dma, dma,
             dma((2, half - 1)), dma((2, half - 1)), dma((2, gy - 1)), dma((2, gy - 1)), dma, dma,
+            dma((2, half - 1)), dma((2, half - 1)), dma((2, gy - 1)), dma((2, gy - 1)),
+            dma((gx - 1,)), dma((gx - 1,)),
         ],
         compiler_params=pltpu.CompilerParams(collective_id=0, has_side_effects=True),
     )(layer_early, layer_late)
-    return small[1, 0], small[0, :rows], early_rows, late_rows
+    early_rows = (early_raw.astype(f32) - early_mean).astype(bf16)
+    late_rows = (layer_late.astype(f32) - late_mean).astype(bf16)
+    return similarity[0, 0], share[0], early_rows, late_rows
 
 
 def fits(gx, gy, tokens, width):
@@ -281,7 +354,7 @@
     cols, rows, block = width // n, tokens // n, tokens // gx
     aligned = cols % 128 == 0 and rows % 16 == 0 and block % 128 == 0
     span = (gx // 2 + 1) * block
-    held = 12 * tokens * cols + 4 * gx * block * span + 24 * block * span
+    held = 20 * tokens * cols + 4 * gx * block * span + 24 * block * span
     return gx % 2 == 0 and gx >= 4 and gy >= 2 and aligned and rows <= block and held <= VMEM_BUDGET
 
 

time: 55.5 us -> 53.7 us (0.968)
  local copies, waits for them, and re-layouts: 4.41 us -> 0.52 us
  other arithmetic: 0 us -> 2.22 us
  Pallas kernels: 50.3 us -> 48.3 us
  between operations: 0.65 us -> 2.42 us
    unnamed x6 -> x5, local copies, waits for them, and re-layouts: 3.38 us -> 0.52 us
    convert_element_type x0 -> x1, other arithmetic: none -> 2.22 us  [exchange_body(): late_rows = (layer_late.astype(f32) - late_mean).astype(bf16)]
    pallas_call x1, Pallas kernels: 50.3 us -> 48.3 us  [exchange_body(): pl.pallas_call(functools.partial(kernel, gx, gy), out_shape=(jax.ShapeDty...]
where the time goes in v2:
time: 53.7 us; the launch traced here: 53.5 us
  Pallas kernels  48.3 us (90%)
  between operations  2.42 us (5%)
  other arithmetic  2.22 us (4%)
    pallas_call x1, Pallas kernels, exchange_body(): pl.pallas_call(functools.partial(kernel, gx, gy), out_shape=(jax.ShapeDty...  48.3 us
    convert_element_type x1, other arithmetic, exchange_body(): late_rows = (layer_late.astype(f32) - late_mean).astype(bf16)  2.22 us

profile of v2, /device:TPU:0, one launch (start us, length us, event | category | flops | bytes accessed | tf_op | source)
XLA Modules:
  0.0 53.5 jit_solution(10868884742296720883)
XLA Ops:
  0.6 0.0 copy-start
  0.6 48.3 %shard_map.57 = (bf16[32,8192]{1,0:T(8,128)(2,1)}, f32[1,8192]{1,0:T(1,128)}, f32[1,8192]{1,0:T(1,128)}, f32[1,32]{1,0:T(1,128)}, f32[1,1]{1,0:T(1,128)}) custom-call(bf16[1024,256]{1,0:T(8,128)(2,1)} %early_hbm.1, bf16[32,8192]{1,0:T(8,128)(2,1)} %late_hbm.1), custom_call_target="tpu_custom_call" | custom-call | tf_op jit(solution)/shard_map/pallas_call | solution.py:315
  49.0 0.0 copy-done
  49.0 2.2 %subtract_convert_fusion = (bf16[32,8192]{1,0:T(8,128)(2,1)}, bf16[32,8192]{1,0:T(8,128)(2,1)}) fusion(bf16[32,8192]{1,0:T(8,128)(2,1)S(1)} %copy-done, f32[8192]{0:T(1024)} %bitcast.5, f32[8192]{0:T(1024)} %bitcast.4, bf16[32,8192]{1,0:T(8,128)(2,1)} %get-tuple-element.11), kind=kLoop, calls=%fused_computation | loop fusion | flops 1572864 | bytes 2162688 | tf_op jit(solution)/shard_map/convert_element_type | solution.py:348
  51.2 0.0 copy-start.1
  51.8 0.0 copy-done.1
  51.8 0.5 copy.9
Async XLA Ops:
  0.6 48.3 %copy-start = (bf16[32,8192]{1,0:T(8,128)(2,1)S(1)}, bf16[32,8192]{1,0:T(8,128)(2,1)}, u32[]{:S(2)}) copy-start(bf16[32,8192]{1,0:T(8,128)(2,1)} %late_hbm.1) | copy-start | bytes 1572868
  51.2 0.6 %copy-start.1 = (f32[1,32]{1,0:T(1,128)S(1)}, f32[1,32]{1,0:T(1,128)}, u32[]{:S(2)}) copy-start(f32[1,32]{1,0:T(1,128)} %get-tuple-element.10) | copy-start | bytes 388

commit v3 on v2

--- a/solution.py
+++ b/solution.py
@@ -242,16 +242,17 @@
     sub = lax.broadcasted_iota(jnp.int32, (rows, block), 0)
     lane = lax.broadcasted_iota(jnp.int32, (rows, block), 1)
     k = final(early_z, early_own, early_zrecv, 0)
-    l = final(late_z, late_own, late_zrecv, 1)
-    kl = k * l
-
     def weighted(v):
         doubled = jnp.sum(v[:, block:half * block])
         return jnp.sum(v[:, :block]) + jnp.sum(v[:, half * block:]) + 2.0 * doubled
 
+    kk = weighted(k * k)
+    l = final(late_z, late_own, late_zrecv, 1)
+    kl = k * l
+
     head = lax.broadcasted_iota(jnp.int32, (1, block), 1)
     scalars = jnp.where(head == 0, weighted(kl), jnp.where(
-        head == 1, weighted(k * k), jnp.where(head == 2, weighted(l * l), 0.0)))
+        head == 1, kk, jnp.where(head == 2, weighted(l * l), 0.0)))
     for d in range(gx):
         if 0 < d < half:
             top = jnp.sum(kl[:, d * block:(d + 1) * block], axis=0, keepdims=True)

time: 53.7 us -> 53.7 us (level)
  no operation moved by 1% of the time
where the time goes in v3:
time: 53.7 us; the launch traced here: 53.5 us
  Pallas kernels  48.3 us (90%)
  between operations  2.42 us (5%)
  other arithmetic  2.22 us (4%)
    pallas_call x1, Pallas kernels, exchange_body(): pl.pallas_call(functools.partial(kernel, gx, gy), out_shape=(jax.ShapeDty...  48.3 us
    convert_element_type x1, other arithmetic, exchange_body(): late_rows = (layer_late.astype(f32) - late_mean).astype(bf16)  2.22 us

profile of v3, /device:TPU:0, one launch (start us, length us, event | category | flops | bytes accessed | tf_op | source)
XLA Modules:
  0.0 53.5 jit_solution(11607209357390893876)
XLA Ops:
  0.6 0.0 copy-start
  0.6 48.3 %shard_map.57 = (bf16[32,8192]{1,0:T(8,128)(2,1)}, f32[1,8192]{1,0:T(1,128)}, f32[1,8192]{1,0:T(1,128)}, f32[1,32]{1,0:T(1,128)}, f32[1,1]{1,0:T(1,128)}) custom-call(bf16[1024,256]{1,0:T(8,128)(2,1)} %early_hbm.1, bf16[32,8192]{1,0:T(8,128)(2,1)} %late_hbm.1), custom_call_target="tpu_custom_call" | custom-call | tf_op jit(solution)/shard_map/pallas_call | solution.py:316
  49.0 0.0 copy-done
  49.0 2.2 %subtract_convert_fusion = (bf16[32,8192]{1,0:T(8,128)(2,1)}, bf16[32,8192]{1,0:T(8,128)(2,1)}) fusion(bf16[32,8192]{1,0:T(8,128)(2,1)S(1)} %copy-done, f32[8192]{0:T(1024)} %bitcast.5, f32[8192]{0:T(1024)} %bitcast.4, bf16[32,8192]{1,0:T(8,128)(2,1)} %get-tuple-element.11), kind=kLoop, calls=%fused_computation | loop fusion | flops 1572864 | bytes 2162688 | tf_op jit(solution)/shard_map/convert_element_type | solution.py:349
  51.2 0.0 copy-start.1
  51.8 0.0 copy-done.1
  51.8 0.5 copy.9
Async XLA Ops:
  0.6 48.3 %copy-start = (bf16[32,8192]{1,0:T(8,128)(2,1)S(1)}, bf16[32,8192]{1,0:T(8,128)(2,1)}, u32[]{:S(2)}) copy-start(bf16[32,8192]{1,0:T(8,128)(2,1)} %late_hbm.1) | copy-start | bytes 1572868
  51.2 0.6 %copy-start.1 = (f32[1,32]{1,0:T(1,128)S(1)}, f32[1,32]{1,0:T(1,128)}, u32[]{:S(2)}) copy-start(f32[1,32]{1,0:T(1,128)} %get-tuple-element.10) | copy-start | bytes 388
